TPU v7x, 32 devices: a whole 2x2x4 slice. The times are simulated.
32 devices in a mesh: dev: 32 (over z, y, x, core).
Axes of the slice: x: 2, y: 2, z: 4, core: 2. Of those that a mesh axis runs over, the one named last changes fastest.
Arguments:
- state_real: float32 [4194304], P('dev'), may hold values from -24 to 24, as said below
- state_imag: float32 [4194304], P('dev'), may hold values from -24 to 24, as said below
- subsystem: int32 [3], replicated, may hold values from 0 to 16, as said below
Outputs:
- rho_real: float32 [256, 256], P('dev')
- rho_imag: float32 [256, 256], P('dev')
Inputs may be any that keep to these rules, and one draw needn't show every extreme that they name: `subsystem`: the 3 entries are distinct local bit positions in ascending order; the first is always 0 and the last always 17 - 1. `state_real`: real parts of amplitudes; their typical size changes between aligned blocks of 2**(11) local indices by up to a factor of 16. `state_imag`: imaginary parts of amplitudes, with the same block sizes as the real parts.
All inputs are finite; a program needn't handle non-finite values.
Results may differ from a plain program's by a relative error of at most 0.0001.
Values sent between devices are 32-bit elements; how exact they have to be, the bound alone decides.
A program may use at most 192 MiB of HBM per device.

v0:
```python
import jax
import jax.numpy as jnp
from jax import lax
from jax.sharding import PartitionSpec as P


def regroup(local_bits):
    branches = []
    for lower_count in range(local_bits - 2):

        def make_branch(flat, lower_count=lower_count):
            upper = 2 ** (local_bits - 3 - lower_count)
            lower = 2**lower_count
            shaped = flat.reshape(2, upper, 2, lower, 2)
            moved = jnp.transpose(shaped, (0, 2, 4, 1, 3))
            return moved.reshape(8, upper * lower)

        branches.append(make_branch)
    return branches


def contract(left, right):
    return lax.dot_general(
        left,
        right,
        (((1,), (1,)), ((), ())),
        precision=lax.Precision.HIGHEST,
        preferred_element_type=jnp.float32,
    )


def gram(left_re, left_im, right_re, right_im):
    joined = jnp.concatenate([right_re, right_im], axis=1)
    left_x = jnp.concatenate([left_re, left_im], axis=1)
    left_y = jnp.concatenate([left_im, -left_re], axis=1)
    product = contract(jnp.concatenate([left_x, left_y], axis=0), joined)
    row_total = left_re.shape[0]
    return (product[:row_total], product[row_total:])


def local(state_real, state_imag, subsystem):
    local_bits = state_real.shape[0].bit_length() - 1
    count_rest = state_real.shape[0] // 8
    branches = regroup(local_bits)
    middle_place = jnp.clip(subsystem[1] - 1, 0, local_bits - 3)
    local_real = lax.switch(middle_place, branches, state_real)
    local_imag = lax.switch(middle_place, branches, state_imag)
    received_re, received_im = (
        lax.all_to_all(local_real, "dev", split_axis=1, concat_axis=0, tiled=True),
        lax.all_to_all(local_imag, "dev", split_axis=1, concat_axis=0, tiled=True),
    )
    full_width = received_re.shape[0]
    scale = 1.0 / count_rest
    left_re = lax.slice_in_dim(received_re, 0, full_width, axis=0)
    left_im = lax.slice_in_dim(received_im, 0, full_width, axis=0)
    real_part, imag_part = gram(left_re, left_im, received_re, received_im)
    own_rows = lax.psum_scatter(
        jnp.concatenate([real_part, imag_part], axis=1), "dev", scatter_dimension=0, tiled=True
    )
    own_rows = own_rows * scale
    return (own_rows[:, :full_width], own_rows[:, full_width:])


def solution(mesh):
    return jax.shard_map(
        local,
        mesh=mesh,
        in_specs=(P("dev"), P("dev"), P()),
        out_specs=(P("dev", None), P("dev", None)),
        check_vma=False,
    )
```

profile of v0, /device:TPU:0, one launch (start us, length us, event | category | flops | bytes accessed | tf_op | source)
XLA Modules:
  0.0 324.3 jit_solution(1908655987549556454)
XLA Ops:
  7.2 1.2 slice.15
  9.1 0.0 copy-start
  9.1 69.1 %conditional.2 = (f32[8,16384]{1,0:T(8,128)}) conditional(s32[]{:T(128)} %bitcast.30, f32[131072]{0:T(1024)} %param.33, f32[131072]{0:T(1024)} %param.33, f32[131072]{0:T(1024)} %param.33, f32[131072]{0:T(1024)} %param.33, f32[131072]{0:T(1024)} %param.33, f32[131072]{0:T(1024)} %param.33, ...), branch_computations={%region_0.1_spmd, %region_1.2_spmd, %region_2.3_spmd, %region_3.4_... | conditional | bytes 3145736 | solution.py:46
  17.4 35.6 %reshape.153 = f32[2,128,2,128,2]{4,3,2,1,0:T(8,128)} reshape(f32[131072]{0:T(1024)} %param.7) | data formatting | bytes 1048576 | tf_op jit(solution)/shard_map/cond/branch_7_fun/reshape | solution.py:14
  53.0 19.5 %copy.60 = f32[2,2,2,128,128]{4,3,2,1,0:T(8,128)S(1)} copy(f32[2,2,2,128,128]{2,4,1,3,0:T(8,128)} %bitcast.127) | data formatting | bytes 1048576 | tf_op jit(solution)/shard_map/cond/branch_7_fun/transpose | solution.py:15
  72.4 1.1 copy.103
  78.2 0.0 copy-done
  78.2 7.5 %all-to-all-start = ((f32[8,32,512]{2,0,1:T(8,128)}), f32[8,32,512]{2,0,1:T(8,128)}, u32[]{:S(2)}, u32[]{:S(2)}) async-start(f32[8,32,512]{2,0,1:T(8,128)} %bitcast.31), calls=%async_computation | async-start | bytes 1048576 | tf_op jit(solution)/shard_map/all_to_all | solution.py:49
  85.7 67.4 %conditional.3 = (f32[8,16384]{1,0:T(8,128)}) conditional(s32[]{:T(128)} %bitcast.30, f32[131072]{0:T(1024)S(1)} %copy-done, f32[131072]{0:T(1024)S(1)} %copy-done, f32[131072]{0:T(1024)S(1)} %copy-done, f32[131072]{0:T(1024)S(1)} %copy-done, f32[131072]{0:T(1024)S(1)} %copy-done, f32[131072]{0:T(1024)S(1)} %copy-done, ...), branch_computations={%region_15.16_spmd, %region_16.17_spmd, %region_17.18_spmd, %regio... | conditional | bytes 3145736 | solution.py:47
  94.8 34.8 %reshape.183 = f32[2,128,2,128,2]{4,3,2,1,0:T(8,128)} reshape(f32[131072]{0:T(1024)S(1)} %param.22) | data formatting | bytes 1048576 | tf_op jit(solution)/shard_map/cond/branch_7_fun/reshape | solution.py:14
  129.6 19.5 %copy.75 = f32[2,2,2,128,128]{4,3,2,1,0:T(8,128)S(1)} copy(f32[2,2,2,128,128]{2,4,1,3,0:T(8,128)} %bitcast.141) | data formatting | bytes 1048576 | tf_op jit(solution)/shard_map/cond/branch_7_fun/transpose | solution.py:15
  149.1 1.1 copy.104
  153.1 0.0 all-to-all-done
  153.1 7.3 %all-to-all-start.1 = ((f32[8,32,512]{2,0,1:T(8,128)}), f32[8,32,512]{2,0,1:T(8,128)S(1)}, u32[]{:S(2)}, u32[]{:S(2)}) async-start(f32[8,32,512]{2,0,1:T(8,128)} %bitcast.34), calls=%async_computation.1 | async-start | bytes 1048576 | tf_op jit(solution)/shard_map/all_to_all | solution.py:50
  160.5 0.0 reduce-scatter.4.cloned.1.call-start
  160.5 1.1 bitcast_negate_fusion
  161.6 14.5 %all-to-all-done.1 = f32[8,32,512]{2,0,1:T(8,128)S(1)} async-done(((f32[8,32,512]{2,0,1:T(8,128)}), f32[8,32,512]{2,0,1:T(8,128)S(1)}, u32[]{:S(2)}, u32[]{:S(2)}) %all-to-all-start.1) | async-done | bytes 524320 | tf_op jit(solution)/shard_map/all_to_all | solution.py:50
  176.1 3.2 fusion
  179.3 1.0 copy.85
  180.3 0.0 reduce-scatter.4.cloned.1.call-update
  180.4 134.2 %reduce-scatter.4.cloned.1.call-done = f32[8,512]{1,0:T(8,128)} async-done(((f32[256,512]{1,0:T(8,128)}), f32[8,512]{1,0:T(8,128)}) %reduce-scatter.4.cloned.1.call-update) | async-done | bytes 16400
  314.6 0.8 copy.86
  315.5 0.7 copy.84
  316.2 0.7 copy.83
  (4 shorter events, 0.1 us)
Async XLA Ops:
  9.1 69.1 %copy-start = (f32[131072]{0:T(1024)S(1)}, f32[131072]{0:T(1024)}, u32[]{:S(2)}) copy-start(f32[131072]{0:T(1024)} %param.34) | copy-start | bytes 1572868
  78.2 74.9 %all-to-all-start = ((f32[8,32,512]{2,0,1:T(8,128)}), f32[8,32,512]{2,0,1:T(8,128)}, u32[]{:S(2)}, u32[]{:S(2)}) async-start(f32[8,32,512]{2,0,1:T(8,128)} %bitcast.31), calls=%async_computation | async-start | bytes 1048576 | tf_op jit(solution)/shard_map/all_to_all | solution.py:49
  153.1 23.0 %all-to-all-start.1 = ((f32[8,32,512]{2,0,1:T(8,128)}), f32[8,32,512]{2,0,1:T(8,128)S(1)}, u32[]{:S(2)}, u32[]{:S(2)}) async-start(f32[8,32,512]{2,0,1:T(8,128)} %bitcast.34), calls=%async_computation.1 | async-start | bytes 1048576 | tf_op jit(solution)/shard_map/all_to_all | solution.py:50
  160.5 154.1 %reduce-scatter.4.cloned.1.call-start = ((), (), s32[]{:S(2)}) async-start(), calls=%async_computation.3 | async-start | bytes 540672
Sparse Core Ops, SparseCore 0:
  180.5 134.0 reduce-scatter.3
where the time goes:
time: 329 us; the launch traced here: 324 us
  waiting for transfers between devices  149 us (45%)
  local copies, waits for them, and re-layouts  116 us (35%)
  loops' own time  24.9 us (8%)
  between operations  15.4 us (5%)
  starting transfers between devices  14.8 us (4%)
    unnamed x2, waiting for transfers between devices  134 us
    reshape x2, local copies, waits for them, and re-layouts, make_branch(): shaped = flat.reshape(2, upper, 2, lower, 2)  70.4 us
    transpose x2, local copies, waits for them, and re-layouts, make_branch(): moved = jnp.transpose(shaped, (0, 2, 4, 1, 3))  39 us
    all_to_all x1, waiting for transfers between devices, local(): lax.all_to_all(local_imag, 'dev', split_axis=1, concat_axis=0, tiled=True)  14.5 us
    another operation x1, loops' own time, local(): local_real = lax.switch(middle_place, branches, state_real)  12.9 us
    another operation x1, loops' own time, local(): local_imag = lax.switch(middle_place, branches, state_imag)  12 us
    all_to_all x1, starting transfers between devices, local(): lax.all_to_all(local_real, 'dev', split_axis=1, concat_axis=0, tiled=True)  7.46 us
    all_to_all x1, starting transfers between devices, local(): lax.all_to_all(local_imag, 'dev', split_axis=1, concat_axis=0, tiled=True)  7.33 us
  transfers between devices with their start and end apart: 3, of which 2 were waited for; matrix products, arithmetic and copies ran while one was open for 17% of the time, Pallas kernels for 0%

commit v1 on v0

--- a/solution.py
+++ b/solution.py
@@ -47,7 +47,12 @@
     local_imag = lax.switch(middle_place, branches, state_imag)
     received_re, received_im = (
         lax.all_to_all(local_real, "dev", split_axis=1, concat_axis=0, tiled=True),
-        lax.all_to_all(local_imag, "dev", split_axis=1, concat_axis=0, tiled=True),
+        jnp.concatenate(
+            lax.all_to_all(
+                jnp.stack(jnp.split(local_imag, lax.axis_size("dev"), axis=1)), "dev", 0, 0
+            ),
+            axis=0,
+        ),
     )
     full_width = received_re.shape[0]
     scale = 1.0 / count_rest

time: 329 us -> 348 us (1.058)
  local copies, waits for them, and re-layouts: 116 us -> 135 us
    unnamed x6 -> x37, local copies, waits for them, and re-layouts: 3.18 us -> 21.8 us
  transfers between devices with their start and end apart: 3 -> 3, of which waited for: 2 -> 2; matrix products, arithmetic and copies ran while one was open for 17% -> 22% of each run, Pallas kernels for 0% -> 0%
where the time goes in v1:
time: 348 us; the launch traced here: 343 us
  waiting for transfers between devices  149 us (43%)
  local copies, waits for them, and re-layouts  135 us (39%)
  loops' own time  25.5 us (7%)
  between operations  15 us (4%)
  starting transfers between devices  14.8 us (4%)
    unnamed x2, waiting for transfers between devices  134 us
    reshape x2, local copies, waits for them, and re-layouts, make_branch(): shaped = flat.reshape(2, upper, 2, lower, 2)  70.5 us
    transpose x2, local copies, waits for them, and re-layouts, make_branch(): moved = jnp.transpose(shaped, (0, 2, 4, 1, 3))  39 us
    unnamed x37, local copies, waits for them, and re-layouts  21.8 us
    all_to_all x1, waiting for transfers between devices, local(): lax.all_to_all(jnp.stack(jnp.split(local_imag, lax.axis_size('dev'), axis...  14.5 us
    another operation x1, loops' own time, local(): local_real = lax.switch(middle_place, branches, state_real)  13 us
    another operation x1, loops' own time, local(): local_imag = lax.switch(middle_place, branches, state_imag)  12.6 us
    all_to_all x1, starting transfers between devices, local(): lax.all_to_all(local_real, 'dev', split_axis=1, concat_axis=0, tiled=True)  7.46 us
  transfers between devices with their start and end apart: 3, of which 2 were waited for; matrix products, arithmetic and copies ran while one was open for 22% of the time, Pallas kernels for 0%

profile of v1, /device:TPU:0, one launch (start us, length us, event | category | flops | bytes accessed | tf_op | source)
XLA Modules:
  0.0 343.1 jit_solution(10182584299049835566)
XLA Ops:
  7.2 1.2 slice.15
  9.1 69.2 %conditional.2 = (f32[8,16384]{1,0:T(8,128)}) conditional(s32[]{:T(128)} %bitcast.510, f32[131072]{0:T(1024)} %param.33, f32[131072]{0:T(1024)} %param.33, f32[131072]{0:T(1024)} %param.33, f32[131072]{0:T(1024)} %param.33, f32[131072]{0:T(1024)} %param.33, f32[131072]{0:T(1024)} %param.33, ...), branch_computations={%region_0.1_spmd, %region_1.2_spmd, %region_2.3_spmd, %region_3.4_... | conditional | bytes 3145736 | solution.py:46
  17.4 35.6 %reshape.182 = f32[2,128,2,128,2]{4,3,2,1,0:T(8,128)} reshape(f32[131072]{0:T(1024)} %param.7) | data formatting | bytes 1048576 | tf_op jit(solution)/shard_map/cond/branch_7_fun/reshape | solution.py:14
  53.0 19.5 %copy.60 = f32[2,2,2,128,128]{4,3,2,1,0:T(8,128)S(1)} copy(f32[2,2,2,128,128]{2,4,1,3,0:T(8,128)} %bitcast.1084) | data formatting | bytes 1048576 | tf_op jit(solution)/shard_map/cond/branch_7_fun/transpose | solution.py:15
  72.5 1.1 copy.103
  78.3 7.5 %all-to-all-start = ((f32[8,32,512]{2,0,1:T(8,128)}), f32[8,32,512]{2,0,1:T(8,128)}, u32[]{:S(2)}, u32[]{:S(2)}) async-start(f32[8,32,512]{2,0,1:T(8,128)} %bitcast.511), calls=%async_computation | async-start | bytes 1048576 | tf_op jit(solution)/shard_map/all_to_all | solution.py:49
  85.8 67.3 %conditional.3 = (f32[1,8,512]{2,1,0:T(8,128)S(1)}, f32[1,8,512]{2,1,0:T(8,128)S(1)}, f32[1,8,512]{2,1,0:T(8,128)S(1)}, f32[1,8,512]{2,1,0:T(8,128)S(1)}, f32[1,...) conditional(s32[]{:T(128)} %bitcast.510, ...), branch_computations={%region_15.16_spmd, %region_16.17_spmd, %region_17.18_spmd, %regio... | conditional | bytes 4194560 | solution.py:47
  95.1 34.9 %reshape.212 = f32[2,128,2,128,2]{4,3,2,1,0:T(8,128)} reshape(f32[131072]{0:T(1024)S(1)} %param.22) | data formatting | bytes 1048576 | tf_op jit(solution)/shard_map/cond/branch_7_fun/reshape | solution.py:14
  129.9 19.5 %copy.75 = f32[2,2,2,128,128]{4,3,2,1,0:T(8,128)S(1)} copy(f32[2,2,2,128,128]{2,4,1,3,0:T(8,128)} %bitcast.1098) | data formatting | bytes 1048576 | tf_op jit(solution)/shard_map/cond/branch_7_fun/transpose | solution.py:15
  153.0 0.6 constant_dynamic-update-slice_fusion.31
  153.6 0.6 constant_dynamic-update-slice_fusion.30
  154.2 0.6 constant_dynamic-update-slice_fusion.29
  154.8 0.6 constant_dynamic-update-slice_fusion.28
  155.4 0.6 constant_dynamic-update-slice_fusion.27
  156.0 0.6 constant_dynamic-update-slice_fusion.26
  156.6 0.6 constant_dynamic-update-slice_fusion.25
  157.2 0.6 constant_dynamic-update-slice_fusion.24
  157.8 0.6 constant_dynamic-update-slice_fusion.23
  158.4 0.6 constant_dynamic-update-slice_fusion.22
  159.0 0.6 constant_dynamic-update-slice_fusion.21
  159.6 0.6 constant_dynamic-update-slice_fusion.20
  160.2 0.6 constant_dynamic-update-slice_fusion.19
  160.8 0.6 constant_dynamic-update-slice_fusion.18
  161.4 0.6 constant_dynamic-update-slice_fusion.17
  162.0 0.6 constant_dynamic-update-slice_fusion.16
  162.6 0.6 constant_dynamic-update-slice_fusion.15
  163.2 0.6 constant_dynamic-update-slice_fusion.14
  164.4 0.6 constant_dynamic-update-slice_fusion.12
  165.0 0.6 constant_dynamic-update-slice_fusion.11
  165.6 0.6 constant_dynamic-update-slice_fusion.10
  166.2 0.6 constant_dynamic-update-slice_fusion.9
  166.8 0.6 constant_dynamic-update-slice_fusion.8
  167.4 0.6 constant_dynamic-update-slice_fusion.7
  168.0 0.6 constant_dynamic-update-slice_fusion.6
  168.6 0.6 constant_dynamic-update-slice_fusion.5
  169.2 0.6 constant_dynamic-update-slice_fusion.4
  169.8 0.6 constant_dynamic-update-slice_fusion.3
  171.0 0.6 constant_dynamic-update-slice_fusion.1
  171.7 0.6 constant_dynamic-update-slice_fusion
  172.3 7.3 %all-to-all-start.1 = ((f32[32,8,512]{2,1,0:T(8,128)}), f32[32,8,512]{2,1,0:T(8,128)S(1)}, u32[]{:S(2)}, u32[]{:S(2)}) async-start(f32[32,8,512]{2,1,0:T(8,128)} %constant_dynamic-update-slice_fusion), calls=%async_computation.1 | async-start | bytes 1048576 | tf_op jit(solution)/shard_map/all_to_all | solution.py:51
  179.6 1.1 bitcast_negate_fusion
  180.7 14.5 %all-to-all-done.1 = f32[32,8,512]{2,1,0:T(8,128)S(1)} async-done(((f32[32,8,512]{2,1,0:T(8,128)}), f32[32,8,512]{2,1,0:T(8,128)S(1)}, u32[]{:S(2)}, u32[]{:S(2)}) %all-to-all-start.1) | async-done | bytes 524320 | tf_op jit(solution)/shard_map/all_to_all | solution.py:51
  195.2 3.2 fusion
  198.5 1.0 copy.85
  199.5 134.3 %reduce-scatter.4.cloned.1.call-done = f32[8,512]{1,0:T(8,128)} async-done(((f32[256,512]{1,0:T(8,128)}), f32[8,512]{1,0:T(8,128)}) %reduce-scatter.4.cloned.1.call-update) | async-done | bytes 16400
  333.8 0.8 copy.86
  334.7 0.7 copy.84
  335.4 0.7 copy.83
  (14 shorter events, 1.7 us)
Async XLA Ops:
  9.1 69.2 %copy-start = (f32[131072]{0:T(1024)S(1)}, f32[131072]{0:T(1024)}, u32[]{:S(2)}) copy-start(f32[131072]{0:T(1024)} %param.34) | copy-start | bytes 1572868
  78.3 94.0 %all-to-all-start = ((f32[8,32,512]{2,0,1:T(8,128)}), f32[8,32,512]{2,0,1:T(8,128)}, u32[]{:S(2)}, u32[]{:S(2)}) async-start(f32[8,32,512]{2,0,1:T(8,128)} %bitcast.511), calls=%async_computation | async-start | bytes 1048576 | tf_op jit(solution)/shard_map/all_to_all | solution.py:49
  172.3 22.9 %all-to-all-start.1 = ((f32[32,8,512]{2,1,0:T(8,128)}), f32[32,8,512]{2,1,0:T(8,128)S(1)}, u32[]{:S(2)}, u32[]{:S(2)}) async-start(f32[32,8,512]{2,1,0:T(8,128)} %constant_dynamic-update-slice_fusion), calls=%async_computation.1 | async-start | bytes 1048576 | tf_op jit(solution)/shard_map/all_to_all | solution.py:51
  179.6 154.2 %reduce-scatter.4.cloned.1.call-start = ((), (), s32[]{:S(2)}) async-start(), calls=%async_computation.3 | async-start | bytes 540672
Sparse Core Ops, SparseCore 0:
  199.6 134.1 reduce-scatter.3
